TPU v7x, 32 devices: a whole 2x2x4 slice. The times are simulated.
32 devices in a mesh: cache: 8 (over z, x), expert: 4 (over y, core).
Axes of the slice: x: 2, y: 2, z: 4, core: 2. Of those that a mesh axis runs over, the one named last changes fastest.
Arguments:
- query: bfloat16 [512, 2048], P('cache', 'expert'), may hold values from -8 to 8
- new_key: bfloat16 [512, 512], P('cache', 'expert'), may hold values from -8 to 8
- new_value: bfloat16 [512, 512], P('cache', 'expert'), may hold values from -6 to 6
- private_keys: bfloat16 [512, 64, 512], P('cache', None, 'expert'), may hold values from -8 to 8
- private_values: bfloat16 [512, 64, 512], P('cache', None, 'expert'), may hold values from -6 to 6
- private_lengths: int32 [512], P('cache'), may hold values from 1 to 64
- prefix_keys: bfloat16 [16, 1024, 512], P('cache', None, 'expert'), may hold values from -8 to 8
- prefix_values: bfloat16 [16, 1024, 512], P('cache', None, 'expert'), may hold values from -6 to 6
- slot_group: int32 [16], replicated, may hold values from 0 to 15, each once
- group_ids: int32 [512, 1], P('cache'), may hold values from 0 to 15; in each aligned block of 64 rows (0 to 63, 64 to 127, ...) at most 8 rows name the same one
- out_weight: bfloat16 [2048, 4096], P('expert', 'cache'), may hold values from -0.125 to 0.125
- hidden_in: bfloat16 [512, 4096], P(('cache', 'expert')), may hold values from -6 to 6
- norm_gain: float32 [4096], replicated, may hold values from 0.1 to 1.9
- expert_ids: int32 [512, 2], P(('cache', 'expert')), may hold values from 0 to 3, all different within a row; in each aligned block of 16 rows (0 to 15, 16 to 31, ...) at most 16 rows name the same one
- gate_weights: float32 [512, 2], P(('cache', 'expert')), may hold values from 0.1 to 0.9
- w_gate: bfloat16 [4, 4096, 14336], P('expert', None, 'cache'), may hold values from -0.09375 to 0.09375
- w_up: bfloat16 [4, 4096, 14336], P('expert', None, 'cache'), may hold values from -0.09375 to 0.09375
- w_down: bfloat16 [4, 14336, 4096], P('expert', 'cache'), may hold values from -0.046875 to 0.046875
Outputs:
- attention: bfloat16 [512, 2048], P('cache', 'expert')
- layer_out: bfloat16 [512, 4096], P(('cache', 'expert'))
Inputs may be any that keep to these rules, and one draw needn't show every extreme that they name: `group_ids`: within each aligned block of 64 requests at most 8 name one group. `slot_group`: each group is held by exactly one slot. `private_lengths`: positions 0 to length - 1 of a request's private cache are live. `expert_ids`: each token names two different experts; among the 16 tokens of one device at most 16 name one expert.
All inputs are finite; a program needn't handle non-finite values.
Results may differ from a plain program's by a relative error of at most 0.0095.
Values may be sent and summed in bfloat16 or wider, within the bound.
A program may use at most 128 MiB of HBM per device.

v0:
```python
import math
import jax
import jax.numpy as jnp
from jax import lax
from jax.sharding import PartitionSpec as P

MOSTG = 8
NEG = -1e30
EPSILON = 1e-05


def private_partial(queries, keys, values, lengths, new_key, new_value, scale):
    scores = jnp.einsum("rhd,rpd->rhp", queries, keys, preferred_element_type=jnp.float32) * scale
    live = jnp.arange(keys.shape[1], dtype=jnp.int32)[None, :] < lengths[:, None]
    scores = jnp.where(live[:, None, :], scores, NEG)
    fresh = jnp.einsum("rhd,rd->rh", queries, new_key, preferred_element_type=jnp.float32) * scale
    top = jnp.maximum(jnp.max(scores, axis=-1), fresh)
    expo = jnp.where(live[:, None, :], jnp.exp(scores - top[..., None]), 0.0)
    fresh_expo = jnp.exp(fresh - top)
    total = jnp.sum(expo, axis=-1) + fresh_expo
    summed = jnp.einsum(
        "rhp,rpd->rhd", expo.astype(jnp.bfloat16), values, preferred_element_type=jnp.float32
    )
    fresh_weight = lax.optimization_barrier(fresh_expo.astype(jnp.bfloat16)).astype(jnp.float32)
    summed = summed + fresh_weight[..., None] * new_value.astype(jnp.float32)[:, None, :]
    return (summed / total[..., None], top + jnp.log(total))


def prefix_partial(received, prefix_keys, prefix_values, scale):
    rows, heads, width = received.shape
    slots = prefix_keys.shape[0]
    blocks = received.reshape(rows // (slots * MOSTG), slots, MOSTG, heads, width)
    scores = (
        jnp.einsum("cgmhd,gpd->cgmhp", blocks, prefix_keys, preferred_element_type=jnp.float32)
        * scale
    )
    top = jnp.max(scores, axis=-1)
    expo = jnp.exp(scores - top[..., None])
    total = jnp.sum(expo, axis=-1)
    summed = jnp.einsum(
        "cgmhp,gpd->cgmhd",
        expo.astype(jnp.bfloat16),
        prefix_values,
        preferred_element_type=jnp.float32,
    )
    outputs = (summed / total[..., None]).reshape(rows, heads, width)
    return (outputs, (top + jnp.log(total)).reshape(rows, heads))


def on_device(
    query,
    new_key,
    new_value,
    private_keys,
    private_values,
    private_lengths,
    prefix_keys,
    prefix_values,
    slot_group,
    group_ids,
    out_weight,
    hidden_in,
    norm_gain,
    expert_ids,
    gate_weights,
    w_gate,
    w_up,
    w_down,
):
    head_dim = new_key.shape[1]
    requests = query.shape[0]
    heads = query.shape[1] // head_dim
    scale = 1.0 / math.sqrt(head_dim)
    queries = query.reshape(requests, heads, head_dim)
    near_out, near_lse = private_partial(
        queries, private_keys, private_values, private_lengths, new_key, new_value, scale
    )
    slot_count = slot_group.shape[0]
    matches = group_ids[:, 0][:, None] == slot_group[None, :]
    slot = jnp.sum(jnp.where(matches, jnp.arange(slot_count, dtype=jnp.int32)[None, :], 0), axis=1)
    order = jnp.arange(requests, dtype=jnp.int32)
    earlier = order[None, :] < order[:, None]
    rank = jnp.sum((slot[:, None] == slot[None, :]) & earlier, axis=1)
    position = slot * MOSTG + rank
    places = jnp.arange(slot_count * MOSTG, dtype=jnp.int32)
    placing = places[:, None] == position[None, :]
    sent = jnp.dot(placing.astype(jnp.bfloat16), query, preferred_element_type=jnp.float32).astype(
        jnp.bfloat16
    )
    sent = sent.reshape(slot_count * MOSTG, heads, head_dim)
    outputs, lse_part = prefix_partial(
        lax.all_to_all(sent, "cache", split_axis=0, concat_axis=0, tiled=True),
        prefix_keys,
        prefix_values,
        scale,
    )
    back_out = lax.all_to_all(outputs, "cache", split_axis=0, concat_axis=0, tiled=True)
    back_lse = lax.all_to_all(lse_part, "cache", split_axis=0, concat_axis=0, tiled=True)
    taking = placing.astype(jnp.float32)
    far_out = jnp.einsum("sr,shd->rhd", taking, back_out, precision=lax.Precision.HIGHEST)
    far_lse = jnp.einsum("sr,sh->rh", taking, back_lse, precision=lax.Precision.HIGHEST)
    both = jnp.logaddexp(near_lse, far_lse)
    merged = (
        near_out * jnp.exp(near_lse - both)[..., None]
        + far_out * jnp.exp(far_lse - both)[..., None]
    )
    attention = merged.astype(jnp.bfloat16).reshape(requests, heads * head_dim)
    experts = lax.axis_size("expert")
    tokens = hidden_in.shape[0]
    terms = jnp.dot(
        lax.all_gather(attention, "cache", axis=0, tiled=True),
        out_weight,
        preferred_element_type=jnp.float32,
    )
    regrouped = lax.all_to_all(
        terms.astype(jnp.bfloat16), "cache", split_axis=0, concat_axis=1, tiled=True
    ).astype(terms.dtype)
    proj = lax.psum_scatter(
        regrouped.astype(jnp.bfloat16), "expert", scatter_dimension=0, tiled=True
    ).astype(jnp.float32)
    resid = hidden_in.astype(jnp.float32) + proj
    normed = (
        resid * lax.rsqrt(jnp.mean(resid * resid, axis=-1, keepdims=True) + EPSILON) * norm_gain
    ).astype(jnp.bfloat16)
    capacity = max(2, 4 * tokens // experts)
    flat_ids = expert_ids.reshape(-1)
    order_ids = jnp.arange(flat_ids.shape[0], dtype=jnp.int32)
    before = order_ids[None, :] < order_ids[:, None]
    slot_rank = jnp.sum((flat_ids[:, None] == flat_ids[None, :]) & before, axis=1)
    destination = flat_ids * capacity + slot_rank
    expert_slots = jnp.arange(experts * capacity, dtype=jnp.int32)
    chosen = (destination[None, :] == expert_slots[:, None]).reshape(experts * capacity, tokens, 2)
    picking = jnp.sum(chosen.astype(jnp.bfloat16), axis=2)
    outgoing = jnp.dot(picking, normed, preferred_element_type=jnp.float32).astype(jnp.bfloat16)
    arrived = lax.all_to_all(outgoing, "expert", split_axis=0, concat_axis=0, tiled=True)
    piece = lax.all_gather(arrived, "cache", axis=0, tiled=True)
    gate = jnp.dot(piece, w_gate[0], preferred_element_type=jnp.float32)
    up = jnp.dot(piece, w_up[0], preferred_element_type=jnp.float32)
    act = (jax.nn.silu(gate) * up).astype(jnp.bfloat16)
    partial_out = jnp.dot(act, w_down[0], preferred_element_type=jnp.float32)
    summed_rows = lax.psum_scatter(
        partial_out.astype(jnp.bfloat16), "cache", scatter_dimension=0, tiled=True
    )
    returned = lax.all_to_all(summed_rows, "expert", split_axis=0, concat_axis=0, tiled=True)
    mixing = jnp.sum(jnp.where(chosen, gate_weights[None, :, :], 0.0), axis=2)
    moe = jnp.einsum(
        "st,sd->td", mixing, returned.astype(jnp.float32), precision=lax.Precision.HIGHEST
    )
    layer_out = (resid + moe).astype(jnp.bfloat16)
    return (attention, layer_out)


def solution(mesh):
    in_specs = (
        P("cache", "expert"),
        P("cache", "expert"),
        P("cache", "expert"),
        P("cache", None, "expert"),
        P("cache", None, "expert"),
        P("cache"),
        P("cache", None, "expert"),
        P("cache", None, "expert"),
        P(),
        P("cache", None),
        P("expert", "cache"),
        P(("cache", "expert"), None),
        P(),
        P(("cache", "expert"), None),
        P(("cache", "expert"), None),
        P("expert", None, "cache"),
        P("expert", None, "cache"),
        P("expert", "cache", None),
    )
    out_specs = (P("cache", "expert"), P(("cache", "expert"), None))
    return jax.shard_map(
        on_device, mesh=mesh, in_specs=in_specs, out_specs=out_specs, check_vma=False
    )
```

profile of v0, /device:TPU:0, one launch (start us, length us, event | category | flops | bytes accessed | tf_op | source)
XLA Modules:
  0.0 354.4 jit_solution(17689900936632118236)
XLA Ops:
  7.2 0.8 select_reduce_fusion.1
  8.0 0.2 convert_reduce_fusion
  8.2 1.1 convolution_convert_fusion.2
  9.4 0.7 reshape.100
  10.1 7.3 %all-to-all-start = ((bf16[128,4,128]{2,1,0:T(4,128)(2,1)}), bf16[128,4,128]{2,1,0:T(4,128)(2,1)S(1)}, u32[]{:S(2)}, u32[]{:S(2)}) async-start(bf16[128,4,128]{2,1,0:T(4,128)(2,1)} %reshape.100), calls=%async_computation | async-start | bytes 262144 | tf_op jit(solution)/shard_map/all_to_all | solution.py:92
  17.3 0.9 reshape.99
  18.2 0.7 iota_compare_fusion.4
  18.9 2.0 fusion.61
  20.9 0.9 fusion.45
  22.0 0.1 copy.110
  22.1 2.6 all-to-all-done
  24.7 1.6 bitcast_reduce_fusion
  26.3 0.5 fusion.17
  26.8 0.7 reshape.109
  27.5 3.4 all-to-all-start.1
  31.0 1.6 fusion.18
  32.6 0.9 copy.121
  33.5 4.1 %all-to-all-done.1 = f32[8,16,4]{1,2,0:T(4,128)S(1)} async-done(((f32[8,16,4]{1,2,0:T(4,128)}), f32[8,16,4]{1,2,0:T(4,128)S(1)}, u32[]{:S(2)}, u32[]{:S(2)}) %all-to-all-start.1) | async-done | bytes 2080 | tf_op jit(solution)/shard_map/all_to_all | solution.py:98
  37.5 3.4 all-to-all-start.2
  41.0 0.2 fusion.35
  41.3 0.1 copy.111
  41.5 0.2 subtract_exponential_fusion.1
  41.8 0.1 copy.113
  41.9 0.1 copy.123
  42.0 0.1 copy.119
  42.1 7.0 %all-to-all-done.2 = f32[128,4,128]{2,1,0:T(4,128)S(1)} async-done(((f32[128,4,128]{2,1,0:T(4,128)}), f32[128,4,128]{2,1,0:T(4,128)S(1)}, u32[]{:S(2)}, u32[]{:S(2)}) %all-to-all-start.2) | async-done | bytes 262176 | tf_op jit(solution)/shard_map/all_to_all | solution.py:97
  49.1 0.2 fusion.30
  49.4 0.5 fusion.23
  49.9 31.7 %all_gather.6 = bf16[512,512]{1,0:T(8,128)(2,1)S(1)} all-gather(bf16[64,512]{1,0:T(8,128)(2,1)S(1)} %bitcast.102), channel_id=1, replica_groups=mesh['cache'=8,'expert'=4] {'cache'}, dimensions={0}, use_global_device_ids=true | all-gather | bytes 589824 | tf_op jit(solution)/shard_map/all_gather | solution.py:111
  81.6 0.4 convolution_convert_fusion.1
  82.0 13.0 %all_to_all.62 = bf16[8,64,512]{2,1,0:T(8,128)(2,1)S(1)} all-to-all(bf16[8,64,512]{2,1,0:T(8,128)(2,1)S(1)} %bitcast.92), channel_id=1, replica_groups=mesh['cache'=8,'expert'=4] {'cache'}, dimensions={0} | all-to-all | bytes 1048576 | tf_op jit(solution)/shard_map/all_to_all | solution.py:115
  95.1 0.8 copy.136
  96.0 0.1 copy.126
  96.1 0.1 eq.80
  96.2 0.2 convert_reduce_fusion.1
  96.4 0.1 copy.127
  96.6 20.2 %reduce-scatter.3.cloned.1.call-done = bf16[16,4096]{1,0:T(8,128)(2,1)} async-done(((bf16[64,4096]{1,0:T(8,128)(2,1)}), bf16[16,4096]{1,0:T(8,128)(2,1)}) %reduce-scatter.3.cloned.1.call-update) | async-done | bytes 131088 | tf_op jit(solution)/shard_map/reduce_scatter | solution.py:118
  116.8 1.1 multiply_reduce_fusion
  117.9 1.2 convolution_convert_fusion
  119.1 11.9 %all_to_all.63 = bf16[4,16,4096]{2,1,0:T(8,128)(2,1)} all-to-all(bf16[4,16,4096]{2,1,0:T(8,128)(2,1)S(1)} %bitcast.96), channel_id=1, replica_groups=mesh['cache'=8,'expert'=4] {'expert'}, dimensions={0} | all-to-all | bytes 1048576 | tf_op jit(solution)/shard_map/all_to_all | solution.py:135
  131.0 0.2 reduce-scatter.5.cloned.1.call-start
  131.3 72.7 %all-gather.2.cloned.1.call-done = bf16[512,4096]{1,0:T(8,128)(2,1)} async-done(((bf16[64,4096]{1,0:T(8,128)(2,1)}), bf16[512,4096]{1,0:T(8,128)(2,1)}) %all-gather.2.cloned.1.call-update) | async-done | bytes 4194320 | tf_op jit(solution)/shard_map/all_gather | solution.py:136
  204.0 14.6 %fusion.4 = f32[512,1792]{1,0:T(8,128)} fusion(bf16[512,4096]{1,0:T(8,128)(2,1)} %all-gather.2.cloned.1.call-done, bf16[1,4096,1792]{2,1,0:T(8,128)(2,1)} %param.33), kind=kOutput, calls=%fused_computation.4 | convolution fusion | flops 7516192768 | bytes 22544384 | tf_op jit(solution)/shard_map/dot_general | solution.py:137
  218.6 28.7 %fusion.6 = bf16[512,4096]{1,0:T(8,128)(2,1)} fusion(bf16[1,1792,4096]{2,1,0:T(8,128)(2,1)} %param.35, f32[512,1792]{1,0:T(8,128)} %fusion.4, bf16[512,4096]{1,0:T(8,128)(2,1)} %all-gather.2.cloned.1.call-done, bf16[1,4096,1792]{2,1,0:T(8,128)(2,1)} %param.34), kind=kOutput, calls=%fused_computation.6 | convolution fusion | flops 15039987712 | bytes 41418752 | tf_op jit(solution)/shard_map/dot_general | solution.py:140
  247.3 87.4 %reduce-scatter.5.cloned.1.call-done = bf16[64,4096]{1,0:T(8,128)(2,1)} async-done(((bf16[512,4096]{1,0:T(8,128)(2,1)}), bf16[64,4096]{1,0:T(8,128)(2,1)}) %reduce-scatter.5.cloned.1.call-update) | async-done | bytes 524304 | tf_op jit(solution)/shard_map/reduce_scatter | solution.py:141
  334.6 3.5 all-to-all-start.5
  338.2 8.7 %all-to-all-done.5 = bf16[4,16,4096]{2,1,0:T(8,128)(2,1)S(1)} async-done(((bf16[4,16,4096]{2,1,0:T(8,128)(2,1)}), bf16[4,16,4096]{2,1,0:T(8,128)(2,1)S(1)}, u32[]{:S(2)}, u32[]{:S(2)}) %all-to-all-start.5) | async-done | bytes 524320 | tf_op jit(solution)/shard_map/all_to_all | solution.py:144
  346.9 1.0 fusion.9
  (43 shorter events, 0.9 us)
Async XLA Ops:
  7.2 42.2 %copy-start = (bf16[64,64,128]{2,1,0:T(8,128)(2,1)S(1)}, bf16[64,64,128]{2,1,0:T(8,128)(2,1)}, u32[]{:S(2)}) copy-start(bf16[64,64,128]{2,1,0:T(8,128)(2,1)} %param.22) | copy-start | bytes 3145732
  10.1 14.6 %all-to-all-start = ((bf16[128,4,128]{2,1,0:T(4,128)(2,1)}), bf16[128,4,128]{2,1,0:T(4,128)(2,1)S(1)}, u32[]{:S(2)}, u32[]{:S(2)}) async-start(bf16[128,4,128]{2,1,0:T(4,128)(2,1)} %reshape.100), calls=%async_computation | async-start | bytes 262144 | tf_op jit(solution)/shard_map/all_to_all | solution.py:92
  26.3 15.2 %copy-start.6 = (bf16[64,128]{1,0:T(8,128)(2,1)S(1)}, bf16[64,128]{1,0:T(8,128)(2,1)}, u32[]{:S(2)}) copy-start(bf16[64,128]{1,0:T(8,128)(2,1)} %param.20) | copy-start | bytes 49156
  27.5 10.0 %all-to-all-start.1 = ((f32[8,16,4]{1,2,0:T(4,128)}), f32[8,16,4]{1,2,0:T(4,128)S(1)}, u32[]{:S(2)}, u32[]{:S(2)}) async-start(f32[8,16,4]{1,2,0:T(4,128)} %reshape.109), calls=%async_computation.1 | async-start | bytes 32768 | tf_op jit(solution)/shard_map/all_to_all | solution.py:98
  32.6 49.0 %copy-start.4 = (bf16[512,512]{1,0:T(8,128)(2,1)S(1)}, bf16[512,512]{1,0:T(8,128)(2,1)}, u32[]{:S(2)}) copy-start(bf16[512,512]{1,0:T(8,128)(2,1)} %param.28) | copy-start | bytes 1572868
  37.5 11.6 %all-to-all-start.2 = ((f32[128,4,128]{2,1,0:T(4,128)}), f32[128,4,128]{2,1,0:T(4,128)S(1)}, u32[]{:S(2)}, u32[]{:S(2)}) async-start(f32[128,4,128]{2,1,0:T(4,128)} %copy.121), calls=%async_computation.2 | async-start | bytes 524288 | tf_op jit(solution)/shard_map/all_to_all | solution.py:97
  41.0 75.8 %reduce-scatter.3.cloned.1.call-start = ((), (), s32[]{:S(2)}) async-start(), calls=%async_computation.8 | async-start | bytes 655360 | tf_op jit(solution)/shard_map/reduce_scatter | solution.py:118
  49.4 46.6 %copy-start.8 = (s32[16,2]{0,1:T(2,128)S(1)}, s32[16,2]{0,1:T(2,128)}, u32[]{:S(2)}) copy-start(s32[16,2]{0,1:T(2,128)} %param.31) | copy-start | bytes 388
  49.4 67.4 %copy-start.2 = (bf16[16,4096]{1,0:T(8,128)(2,1)S(1)}, bf16[16,4096]{1,0:T(8,128)(2,1)}, u32[]{:S(2)}) copy-start(bf16[16,4096]{1,0:T(8,128)(2,1)} %param.29) | copy-start | bytes 393220
  49.4 68.4 %copy-start.7 = (f32[4096]{0:T(1024)S(1)}, f32[4096]{0:T(1024)}, u32[]{:S(2)}) copy-start(f32[4096]{0:T(1024)} %param.30) | copy-start | bytes 49156
  49.9 81.1 %copy-start.5 = (bf16[8,8,4,128]{3,1,2,0:T(8,128)(2,1)}, bf16[8,8,4,128]{3,1,2,0:T(8,128)(2,1)S(1)}, u32[]{:S(2)}) copy-start(bf16[8,8,4,128]{3,1,2,0:T(8,128)(2,1)S(1)} %copy.150) | copy-start | bytes 196612
  95.9 108.0 %all-gather.2.cloned.1.call-start = ((), (), s32[]{:S(2)}) async-start(), calls=%async_computation.9 | async-start | bytes 4718592 | tf_op jit(solution)/shard_map/all_gather | solution.py:136
  131.0 203.6 %reduce-scatter.5.cloned.1.call-start = ((), (), s32[]{:S(2)}) async-start(), calls=%async_computation.10 | async-start | bytes 4718592 | tf_op jit(solution)/shard_map/reduce_scatter | solution.py:141
  218.6 129.3 %copy-start.1 = (bf16[64,64,128]{2,1,0:T(8,128)(2,1)S(1)}, bf16[64,64,128]{2,1,0:T(8,128)(2,1)}, u32[]{:S(2)}) copy-start(bf16[64,64,128]{2,1,0:T(8,128)(2,1)} %param.22) | copy-start | bytes 3145732
  247.2 90.9 %copy-start.9 = (f32[16,2]{0,1:T(2,128)S(1)}, f32[16,2]{0,1:T(2,128)}, u32[]{:S(2)}) copy-start(f32[16,2]{0,1:T(2,128)} %param.32) | copy-start | bytes 388
  247.2 99.7 %copy-start.3 = (bf16[16,4096]{1,0:T(8,128)(2,1)S(1)}, bf16[16,4096]{1,0:T(8,128)(2,1)}, u32[]{:S(2)}) copy-start(bf16[16,4096]{1,0:T(8,128)(2,1)} %reduce-scatter.3.cloned.1.call-done) | copy-start | bytes 393220
  334.6 12.3 %all-to-all-start.5 = ((bf16[4,16,4096]{2,1,0:T(8,128)(2,1)}), bf16[4,16,4096]{2,1,0:T(8,128)(2,1)S(1)}, u32[]{:S(2)}, u32[]{:S(2)}) async-start(bf16[4,16,4096]{2,1,0:T(8,128)(2,1)} %bitcast.100), calls=%async_computation.7 | async-start | bytes 1048576 | tf_op jit(solution)/shard_map/all_to_all | solution.py:144
Sparse Core Ops, SparseCore 0:
  96.0 20.6 reduce-scatter.2
  131.2 72.7 all-gather.1
  247.4 87.2 reduce-scatter.4
where the time goes:
time: 355 us; the launch traced here: 354 us
  waiting for transfers between devices  203 us (57%)
  blocking collectives  56.6 us (16%)
  matrix products  54 us (15%)
  starting transfers between devices  17.9 us (5%)
  between operations  14 us (4%)
  local copies, waits for them, and re-layouts  5.2 us (1%)
  other arithmetic  3.97 us (1%)
    reduce_scatter x1, waiting for transfers between devices, on_device(): lax.psum_scatter(partial_out.astype(jnp.bfloat16), 'cache', scatter_dimen...  87.4 us
    all_gather x1, waiting for transfers between devices, on_device(): piece = lax.all_gather(arrived, 'cache', axis=0, tiled=True)  72.7 us
    all_gather x1, blocking collectives, on_device(): lax.all_gather(attention, 'cache', axis=0, tiled=True)  31.7 us
    dot_general x1, matrix products, on_device(): partial_out = jnp.dot(act, w_down[0], preferred_element_type=jnp.float32)  28.7 us
    reduce_scatter x1, waiting for transfers between devices, on_device(): lax.psum_scatter(regrouped.astype(jnp.bfloat16), 'expert', scatter_dimens...  20.2 us
    dot_general x1, matrix products, on_device(): gate = jnp.dot(piece, w_gate[0], preferred_element_type=jnp.float32)  14.6 us
    all_to_all x1, blocking collectives, on_device(): lax.all_to_all(terms.astype(jnp.bfloat16), 'cache', split_axis=0, concat_...  13 us
    all_to_all x1, blocking collectives, on_device(): lax.all_to_all(outgoing, 'expert', split_axis=0, concat_axis=0, tiled=True)  11.9 us
  transfers between devices with their start and end apart: 7, of which 7 were waited for; matrix products, arithmetic and copies ran while one was open for 2% of the time, Pallas kernels for 0%

commit v1 on v0

--- a/solution.py
+++ b/solution.py
@@ -133,7 +133,9 @@
     picking = jnp.sum(chosen.astype(jnp.bfloat16), axis=2)
     outgoing = jnp.dot(picking, normed, preferred_element_type=jnp.float32).astype(jnp.bfloat16)
     arrived = lax.all_to_all(outgoing, "expert", split_axis=0, concat_axis=0, tiled=True)
-    piece = lax.all_gather(arrived, "cache", axis=0, tiled=True)
+    piece = jnp.concatenate(
+        lax.all_to_all(jnp.stack([arrived] * lax.axis_size("cache")), "cache", 0, 0), axis=0
+    )
     gate = jnp.dot(piece, w_gate[0], preferred_element_type=jnp.float32)
     up = jnp.dot(piece, w_up[0], preferred_element_type=jnp.float32)
     act = (jax.nn.silu(gate) * up).astype(jnp.bfloat16)

time: 355 us -> 380 us (1.070)
  blocking collectives: 56.6 us -> 154 us
  waiting for transfers between devices: 203 us -> 129 us
    all_to_all x0 -> x1, blocking collectives: none -> 98.4 us  [on_device(): lax.all_to_all(jnp.stack([arrived] * lax.axis_size('cache')), 'cache', 0, 0)]
    all_gather x1 -> x0, waiting for transfers between devices: 72.7 us -> none  [on_device(): piece = lax.all_gather(arrived, 'cache', axis=0, tiled=True)]
  transfers between devices with their start and end apart: 7 -> 6, of which waited for: 7 -> 6; matrix products, arithmetic and copies ran while one was open for 2% -> 2% of each run, Pallas kernels for 0% -> 0%
where the time goes in v1:
time: 380 us; the launch traced here: 379 us
  blocking collectives  154 us (41%)
  waiting for transfers between devices  129 us (34%)
  matrix products  52.3 us (14%)
  starting transfers between devices  17.7 us (5%)
  between operations  14.3 us (4%)
  local copies, waits for them, and re-layouts  7.69 us (2%)
  other arithmetic  3.97 us (1%)
    all_to_all x1, blocking collectives, on_device(): lax.all_to_all(jnp.stack([arrived] * lax.axis_size('cache')), 'cache', 0, 0)  98.4 us
    reduce_scatter x1, waiting for transfers between devices, on_device(): lax.psum_scatter(partial_out.astype(jnp.bfloat16), 'cache', scatter_dimen...  86.6 us
    all_gather x1, blocking collectives, on_device(): lax.all_gather(attention, 'cache', axis=0, tiled=True)  31.7 us
    dot_general x1, matrix products, on_device(): partial_out = jnp.dot(act, w_down[0], preferred_element_type=jnp.float32)  28.6 us
    reduce_scatter x1, waiting for transfers between devices, on_device(): lax.psum_scatter(regrouped.astype(jnp.bfloat16), 'expert', scatter_dimens...  20.2 us
    all_to_all x1, blocking collectives, on_device(): lax.all_to_all(terms.astype(jnp.bfloat16), 'cache', split_axis=0, concat_...  13 us
    dot_general x1, matrix products, on_device(): gate = jnp.dot(piece, w_gate[0], preferred_element_type=jnp.float32)  12.9 us
    all_to_all x1, blocking collectives, on_device(): lax.all_to_all(outgoing, 'expert', split_axis=0, concat_axis=0, tiled=True)  11.2 us
  transfers between devices with their start and end apart: 6, of which 6 were waited for; matrix products, arithmetic and copies ran while one was open for 2% of the time, Pallas kernels for 0%

profile of v1, /device:TPU:0, one launch (start us, length us, event | category | flops | bytes accessed | tf_op | source)
XLA Modules:
  0.0 379.5 jit_solution(8309466534994313140)
XLA Ops:
  7.2 0.8 select_reduce_fusion.1
  8.0 0.2 convert_reduce_fusion
  8.2 1.1 convolution_convert_fusion.2
  9.4 0.7 reshape.106
  10.1 7.3 %all-to-all-start = ((bf16[128,4,128]{2,1,0:T(4,128)(2,1)}), bf16[128,4,128]{2,1,0:T(4,128)(2,1)S(1)}, u32[]{:S(2)}, u32[]{:S(2)}) async-start(bf16[128,4,128]{2,1,0:T(4,128)(2,1)} %reshape.106), calls=%async_computation | async-start | bytes 262144 | tf_op jit(solution)/shard_map/all_to_all | solution.py:92
  17.3 0.9 reshape.105
  18.2 0.7 iota_compare_fusion.4
  18.9 2.0 fusion.61
  20.9 0.9 fusion.45
  22.0 0.1 copy.110
  22.1 2.6 all-to-all-done
  24.7 1.6 bitcast_reduce_fusion
  26.3 0.5 fusion.17
  26.8 0.7 reshape.116
  27.5 3.4 all-to-all-start.1
  31.0 1.6 fusion.18
  32.6 0.9 copy.121
  33.5 4.1 %all-to-all-done.1 = f32[8,16,4]{1,2,0:T(4,128)S(1)} async-done(((f32[8,16,4]{1,2,0:T(4,128)}), f32[8,16,4]{1,2,0:T(4,128)S(1)}, u32[]{:S(2)}, u32[]{:S(2)}) %all-to-all-start.1) | async-done | bytes 2080 | tf_op jit(solution)/shard_map/all_to_all | solution.py:98
  37.5 3.4 all-to-all-start.2
  41.0 0.2 fusion.35
  41.3 0.1 copy.111
  41.5 0.2 subtract_exponential_fusion.1
  41.8 0.1 copy.113
  41.9 0.1 copy.123
  42.0 0.1 copy.119
  42.1 7.0 %all-to-all-done.2 = f32[128,4,128]{2,1,0:T(4,128)S(1)} async-done(((f32[128,4,128]{2,1,0:T(4,128)}), f32[128,4,128]{2,1,0:T(4,128)S(1)}, u32[]{:S(2)}, u32[]{:S(2)}) %all-to-all-start.2) | async-done | bytes 262176 | tf_op jit(solution)/shard_map/all_to_all | solution.py:97
  49.1 0.2 fusion.30
  49.4 0.5 fusion.23
  49.9 31.7 %all_gather.3 = bf16[512,512]{1,0:T(8,128)(2,1)S(1)} all-gather(bf16[64,512]{1,0:T(8,128)(2,1)S(1)} %bitcast.105), channel_id=1, replica_groups=mesh['cache'=8,'expert'=4] {'cache'}, dimensions={0}, use_global_device_ids=true | all-gather | bytes 589824 | tf_op jit(solution)/shard_map/all_gather | solution.py:111
  81.6 0.4 convolution_convert_fusion.1
  82.0 13.0 %all_to_all.64 = bf16[8,64,512]{2,1,0:T(8,128)(2,1)S(1)} all-to-all(bf16[8,64,512]{2,1,0:T(8,128)(2,1)S(1)} %bitcast.95), channel_id=1, replica_groups=mesh['cache'=8,'expert'=4] {'cache'}, dimensions={0} | all-to-all | bytes 1048576 | tf_op jit(solution)/shard_map/all_to_all | solution.py:115
  95.1 0.8 copy.136
  96.1 0.1 eq.80
  96.2 0.2 convert_reduce_fusion.1
  96.4 0.1 copy.127
  96.6 20.2 %reduce-scatter.3.cloned.1.call-done = bf16[16,4096]{1,0:T(8,128)(2,1)} async-done(((bf16[64,4096]{1,0:T(8,128)(2,1)}), bf16[16,4096]{1,0:T(8,128)(2,1)}) %reduce-scatter.3.cloned.1.call-update) | async-done | bytes 131088 | tf_op jit(solution)/shard_map/reduce_scatter | solution.py:118
  116.8 1.1 multiply_reduce_fusion
  117.9 1.2 convolution_convert_fusion
  119.1 11.2 %all_to_all.65 = bf16[4,16,4096]{2,1,0:T(8,128)(2,1)S(1)} all-to-all(bf16[4,16,4096]{2,1,0:T(8,128)(2,1)S(1)} %bitcast.99), channel_id=1, replica_groups=mesh['cache'=8,'expert'=4] {'expert'}, dimensions={0} | all-to-all | bytes 1048576 | tf_op jit(solution)/shard_map/all_to_all | solution.py:135
  130.4 0.5 stack.5
  130.9 98.4 %all_to_all.66 = bf16[8,64,4096]{2,1,0:T(8,128)(2,1)S(1)} all-to-all(bf16[8,64,4096]{2,1,0:T(8,128)(2,1)S(1)} %stack.5), channel_id=1, replica_groups=mesh['cache'=8,'expert'=4] {'cache'}, dimensions={0} | all-to-all | bytes 8388608 | tf_op jit(solution)/shard_map/all_to_all | solution.py:137
  229.3 2.0 copy-done.2
  231.2 12.9 %fusion.4 = f32[512,1792]{1,0:T(8,128)} fusion(bf16[512,4096]{1,0:T(8,128)(2,1)S(1)} %bitcast.93, bf16[1,4096,1792]{2,1,0:T(8,128)(2,1)} %param.33), kind=kOutput, calls=%fused_computation.4 | convolution fusion | flops 7516192768 | bytes 22544384 | tf_op jit(solution)/shard_map/dot_general | solution.py:139
  244.1 28.6 %fusion.6 = bf16[512,4096]{1,0:T(8,128)(2,1)} fusion(bf16[1,1792,4096]{2,1,0:T(8,128)(2,1)} %param.35, f32[512,1792]{1,0:T(8,128)} %fusion.4, bf16[512,4096]{1,0:T(8,128)(2,1)} %bitcast.94, bf16[1,4096,1792]{2,1,0:T(8,128)(2,1)} %param.34), kind=kOutput, calls=%fused_computation.6 | convolution fusion | flops 15039987712 | bytes 41418752 | tf_op jit(solution)/shard_map/dot_general | solution.py:142
  272.8 86.6 %reduce-scatter.5.cloned.1.call-done = bf16[64,4096]{1,0:T(8,128)(2,1)} async-done(((bf16[512,4096]{1,0:T(8,128)(2,1)}), bf16[64,4096]{1,0:T(8,128)(2,1)}) %reduce-scatter.5.cloned.1.call-update) | async-done | bytes 524304 | tf_op jit(solution)/shard_map/reduce_scatter | solution.py:143
  359.4 3.5 all-to-all-start.6
  363.0 8.7 %all-to-all-done.6 = bf16[4,16,4096]{2,1,0:T(8,128)(2,1)S(1)} async-done(((bf16[4,16,4096]{2,1,0:T(8,128)(2,1)}), bf16[4,16,4096]{2,1,0:T(8,128)(2,1)S(1)}, u32[]{:S(2)}, u32[]{:S(2)}) %all-to-all-start.6) | async-done | bytes 524320 | tf_op jit(solution)/shard_map/all_to_all | solution.py:146
  371.7 1.0 fusion.9
  (44 shorter events, 0.9 us)
Async XLA Ops:
  7.2 42.2 %copy-start = (bf16[64,64,128]{2,1,0:T(8,128)(2,1)S(1)}, bf16[64,64,128]{2,1,0:T(8,128)(2,1)}, u32[]{:S(2)}) copy-start(bf16[64,64,128]{2,1,0:T(8,128)(2,1)} %param.22) | copy-start | bytes 3145732
  10.1 14.6 %all-to-all-start = ((bf16[128,4,128]{2,1,0:T(4,128)(2,1)}), bf16[128,4,128]{2,1,0:T(4,128)(2,1)S(1)}, u32[]{:S(2)}, u32[]{:S(2)}) async-start(bf16[128,4,128]{2,1,0:T(4,128)(2,1)} %reshape.106), calls=%async_computation | async-start | bytes 262144 | tf_op jit(solution)/shard_map/all_to_all | solution.py:92
  26.3 15.2 %copy-start.7 = (bf16[64,128]{1,0:T(8,128)(2,1)S(1)}, bf16[64,128]{1,0:T(8,128)(2,1)}, u32[]{:S(2)}) copy-start(bf16[64,128]{1,0:T(8,128)(2,1)} %param.20) | copy-start | bytes 49156
  27.5 10.0 %all-to-all-start.1 = ((f32[8,16,4]{1,2,0:T(4,128)}), f32[8,16,4]{1,2,0:T(4,128)S(1)}, u32[]{:S(2)}, u32[]{:S(2)}) async-start(f32[8,16,4]{1,2,0:T(4,128)} %reshape.116), calls=%async_computation.1 | async-start | bytes 32768 | tf_op jit(solution)/shard_map/all_to_all | solution.py:98
  32.5 49.0 %copy-start.5 = (bf16[512,512]{1,0:T(8,128)(2,1)S(1)}, bf16[512,512]{1,0:T(8,128)(2,1)}, u32[]{:S(2)}) copy-start(bf16[512,512]{1,0:T(8,128)(2,1)} %param.28) | copy-start | bytes 1572868
  37.5 11.6 %all-to-all-start.2 = ((f32[128,4,128]{2,1,0:T(4,128)}), f32[128,4,128]{2,1,0:T(4,128)S(1)}, u32[]{:S(2)}, u32[]{:S(2)}) async-start(f32[128,4,128]{2,1,0:T(4,128)} %copy.121), calls=%async_computation.2 | async-start | bytes 524288 | tf_op jit(solution)/shard_map/all_to_all | solution.py:97
  41.0 75.8 %reduce-scatter.3.cloned.1.call-start = ((), (), s32[]{:S(2)}) async-start(), calls=%async_computation.9 | async-start | bytes 655360 | tf_op jit(solution)/shard_map/reduce_scatter | solution.py:118
  49.4 46.6 %copy-start.9 = (s32[16,2]{0,1:T(2,128)S(1)}, s32[16,2]{0,1:T(2,128)}, u32[]{:S(2)}) copy-start(s32[16,2]{0,1:T(2,128)} %param.31) | copy-start | bytes 388
  49.4 67.4 %copy-start.3 = (bf16[16,4096]{1,0:T(8,128)(2,1)S(1)}, bf16[16,4096]{1,0:T(8,128)(2,1)}, u32[]{:S(2)}) copy-start(bf16[16,4096]{1,0:T(8,128)(2,1)} %param.29) | copy-start | bytes 393220
  49.4 68.5 %copy-start.8 = (f32[4096]{0:T(1024)S(1)}, f32[4096]{0:T(1024)}, u32[]{:S(2)}) copy-start(f32[4096]{0:T(1024)} %param.30) | copy-start | bytes 49156
  49.9 81.0 %copy-start.6 = (bf16[8,8,4,128]{3,1,2,0:T(8,128)(2,1)}, bf16[8,8,4,128]{3,1,2,0:T(8,128)(2,1)S(1)}, u32[]{:S(2)}) copy-start(bf16[8,8,4,128]{3,1,2,0:T(8,128)(2,1)S(1)} %copy.150) | copy-start | bytes 196612
  95.9 263.5 %reduce-scatter.5.cloned.1.call-start = ((), (), s32[]{:S(2)}) async-start(), calls=%async_computation.10 | async-start | bytes 4718592 | tf_op jit(solution)/shard_map/reduce_scatter | solution.py:143
  229.2 2.0 copy-start.2
  244.1 128.5 %copy-start.1 = (bf16[64,64,128]{2,1,0:T(8,128)(2,1)S(1)}, bf16[64,64,128]{2,1,0:T(8,128)(2,1)}, u32[]{:S(2)}) copy-start(bf16[64,64,128]{2,1,0:T(8,128)(2,1)} %param.22) | copy-start | bytes 3145732
  272.8 90.1 %copy-start.10 = (f32[16,2]{0,1:T(2,128)S(1)}, f32[16,2]{0,1:T(2,128)}, u32[]{:S(2)}) copy-start(f32[16,2]{0,1:T(2,128)} %param.32) | copy-start | bytes 388
  272.8 98.9 %copy-start.4 = (bf16[16,4096]{1,0:T(8,128)(2,1)S(1)}, bf16[16,4096]{1,0:T(8,128)(2,1)}, u32[]{:S(2)}) copy-start(bf16[16,4096]{1,0:T(8,128)(2,1)} %reduce-scatter.3.cloned.1.call-done) | copy-start | bytes 393220
  359.4 12.3 %all-to-all-start.6 = ((bf16[4,16,4096]{2,1,0:T(8,128)(2,1)}), bf16[4,16,4096]{2,1,0:T(8,128)(2,1)S(1)}, u32[]{:S(2)}, u32[]{:S(2)}) async-start(bf16[4,16,4096]{2,1,0:T(8,128)(2,1)} %bitcast.103), calls=%async_computation.8 | async-start | bytes 1048576 | tf_op jit(solution)/shard_map/all_to_all | solution.py:146
Sparse Core Ops, SparseCore 0:
  96.0 20.7 reduce-scatter.2
  272.9 86.4 reduce-scatter.4
